TPU v7x, 256 devices: a whole 4x4x8 slice. The times are simulated.
256 devices in a mesh: clusters: 8 (over y, x_hi), members: 32 (over z, x_lo, core).
Axes of the slice: x: 4 (x_hi: 2, x_lo: 2; x = x_hi * 2 + x_lo), y: 4, z: 8, core: 2. Of those that a mesh axis runs over, the one named last changes fastest.
Arguments:
- embeddings: float32 [131072, 1024], P(('clusters', 'members')), parts along dimension 0, as said below
- member_order: int32 [131072], P(('clusters', 'members')), parts along dimension 0, may hold values from 0 to 16383, each once
- threshold: float32 [8], P('clusters'), parts along dimension 0, may hold values from 0.25 to 0.5
Outputs:
- best_similarity: float32 [131072], P(('clusters', 'members')), parts along dimension 0
- excess: float32 [131072], P(('clusters', 'members')), parts along dimension 0
There are 8 independent parts, one for each index of `clusters`. A program takes and returns all parts, laid end to end along the dimension named above; each array names one. Nothing has to cross between parts.
Inputs may be any that keep to these rules, and one draw needn't show every extreme that they name: member_order holds each of 0 to 16383 once. real-valued embeddings.
All inputs are finite; a program needn't handle non-finite values.
Results may differ from a plain program's by a relative error of at most 0.00051.
Values may be sent and summed in bfloat16 or wider, within the bound.
A program may use at most 128 MiB of HBM per device.

v0:
```python
import jax
import jax.numpy as jnp
from jax import lax
from jax.sharding import PartitionSpec as P


def block_scores(unit, other):
    return lax.dot_general(
        unit, other, (((1,), (1,)), ((), ())), preferred_element_type=jnp.float32
    )


def shards(embeddings, member_order, threshold):
    unit = (
        embeddings * lax.rsqrt(jnp.sum(embeddings * embeddings, axis=1, keepdims=True) + 1e-06)
    ).astype(jnp.bfloat16)
    floor_value = jnp.float32(-1.0)
    start_best = jnp.full((unit.shape[0],), -1.0, jnp.float32)
    scores = block_scores(unit, lax.all_gather(unit, "members", axis=0, tiled=True))
    mask = (
        lax.all_gather(member_order, "members", axis=0, tiled=True)[None, :] < member_order[:, None]
    )
    best = jnp.maximum(start_best, jnp.max(jnp.where(mask, scores, floor_value), axis=1))
    excess = jnp.maximum(best - threshold[0], jnp.float32(0.0))
    return (best, excess)


def solution(mesh):
    placed = (P(("clusters", "members"), None), P(("clusters", "members")), P("clusters"))
    return jax.shard_map(
        shards,
        mesh=mesh,
        in_specs=placed,
        out_specs=(P(("clusters", "members")), P(("clusters", "members"))),
        check_vma=False,
    )
```

profile of v0, /device:TPU:1, one launch (start us, length us, event | category | flops | bytes accessed | tf_op | source)
XLA Modules:
  0.0 231.1 jit_solution(13599985710889065328)
XLA Ops:
  7.2 0.0 all-gather.3.cloned.1.call-start
  7.2 1.8 multiply_reduce_fusion
  9.0 2.8 %multiply_convert_fusion = bf16[512,1024]{1,0:T(8,128)(2,1)} fusion(f32[512,1024]{1,0:T(8,128)} %param.3, f32[512]{0:T(512)S(1)} %add_rsqrt_fusion), kind=kLoop, calls=%fused_computation.1 | loop fusion | flops 1048576 | bytes 3147776 | tf_op jit(solution)/shard_map/convert_element_type | solution.py:16
  11.8 0.0 all-gather.3.cloned.1.call-update
  12.5 39.5 %all-gather = s32[32,1,512]{2,1,0:T(1,128)S(1)} all-gather(s32[1,1,512]{2,1,0:T(1,128)} %bitcast.7), channel_id=1, replica_groups=mesh['clusters'=8,'members'=32] {'members'}, dimensions={0}, use_global_device_ids=true | all-gather | bytes 67584 | tf_op jit(solution)/shard_map/all_gather | solution.py:21
  51.9 148.5 %all-gather.3.cloned.1.call-done = bf16[16384,1024]{1,0:T(8,128)(2,1)} async-done(((bf16[512,1024]{1,0:T(8,128)(2,1)}), bf16[16384,1024]{1,0:T(8,128)(2,1)}) %all-gather.3.cloned.1.call-update) | async-done | bytes 33554448 | tf_op jit(solution)/shard_map/all_gather | solution.py:19
  200.5 23.2 %select_reduce_fusion = f32[512]{0:T(512)S(1)} fusion(bf16[512,1024]{1,0:T(8,128)(2,1)} %multiply_convert_fusion, bf16[16384,1024]{1,0:T(8,128)(2,1)} %all-gather.3.cloned.1.call-done, s32[16384]{0:T(1024)S(1)} %bitcast.6, s32[512]{0:T(512)} %param.4), kind=kOutput, calls=%fused_computation | convolution fusion | flops 17205035008 | bytes 34672640 | tf_op jit(solution)/shard_map/dot_general | solution.py:8
  223.7 0.6 subtract_maximum_fusion
  (1 shorter events, 0.0 us)
Async XLA Ops:
  7.2 193.3 %all-gather.3.cloned.1.call-start = ((), (), s32[]{:S(2)}) async-start(), calls=%async_computation | async-start | bytes 34603008 | tf_op jit(solution)/shard_map/all_gather | solution.py:19
Sparse Core Ops, SparseCore 0:
  11.9 188.4 all-gather.2
where the time goes:
time: 231 us
  waiting for transfers between devices  149 us (65%)
  blocking collectives  39.5 us (17%)
  matrix products  23.2 us (10%)
  between operations  14.7 us (6%)
  other arithmetic  5.16 us (2%)
    all_gather x1, waiting for transfers between devices, shards(): lax.all_gather(unit, 'members', axis=0, tiled=True)  149 us
    all_gather x1, blocking collectives, shards(): lax.all_gather(member_order, 'members', axis=0, tiled=True)[None, :]  39.5 us
    dot_general x1, matrix products, block_scores(): lax.dot_general(unit, other, (((1,), (1,)), ((), ())), preferred_element_...  23.2 us
  transfers between devices with their start and end apart: 1, of which 1 were waited for; matrix products, arithmetic and copies ran while one was open for 0% of the time, Pallas kernels for 0%

commit v1 on v0

v1 whole, which is shorter than its diff:
```python
import functools

import jax
import jax.numpy as jnp
from jax import lax
from jax.experimental import pallas as pl
from jax.experimental.pallas import tpu as pltpu
from jax.sharding import PartitionSpec as P

MESH = pl.DeviceIdType.MESH
F32 = jnp.float32
BF16 = jnp.bfloat16

SO, SP1, SM1, SM2, SP2 = range(5)
BO, BX1, BP2, BXH, NB = 0, 4, 8, 12, 14
DM1, DP1, DOO, DM2, DP2, DX1, DXH, DP2O, DX1O, DXHO, ND = range(11)
VO, VP1, VM1, VM2, VP2, VX1, VXH, NV = 0, 2, 3, 4, 5, 7, 9, 11
RP1, RM1, RM2, RP2, RX1, RXHM, RXHP, NR = 0, 1, 2, 3, 5, 7, 9, 11
NC = 4


def kernel(
    order_ref, thr_ref, emb_ref, out_ref,
    stage, abuf, bbuf, racc, cacc, oa, ob, ordv, res, resin, fin,
    load_sem, send_sem, recv_sem, osend_sem, orecv_sem, rsend_sem, rrecv_sem,
):
    n = lax.axis_size("members")
    nz = n // 4
    me = lax.axis_index("members")
    z, x, c = me // 4, lax.rem(me // 2, 2), lax.rem(me, 2)
    xo, co = 1 - x, 1 - c
    ch = abuf.shape[1] // NC

    def dev(dz, px, pc):
        return {"members": lax.rem(z + dz + nz, nz) * 4 + px * 2 + pc}

    zq = lax.rem(z + 2, nz)
    upper = zq < nz // 2
    low = z < nz // 2

    loads = [
        pltpu.make_async_copy(emb_ref.at[pl.ds(j * ch, ch)], stage.at[j], load_sem.at[j]) for j in range(NC)
    ]
    for j in (0, 2, 1, 3):
        loads[j].start()

    peers = [dev(1, x, c), dev(-1, x, c), dev(0, x, co), dev(0, xo, c)]
    for h in (0, 1):
        peers += [dev(2, x, h), dev(-2, x, h), dev(2, xo, h), dev(-2, xo, h), dev(1, xo, h), dev(-1, xo, h)]
    barrier = pltpu.get_barrier_semaphore()
    for p in peers:
        pl.semaphore_signal(barrier, inc=1, device_id=p, device_id_type=MESH)

    def remote(kind, j, src, dst, target):
        return pltpu.make_async_remote_copy(
            src_ref=src, dst_ref=dst, send_sem=send_sem.at[kind, j], recv_sem=recv_sem.at[kind, j],
            device_id=target, device_id_type=MESH,
        )

    def rows(slot, j):
        return abuf.at[slot, pl.ds(pl.multiple_of(j * ch, ch), ch)]

    def half(tile, h):
        return bbuf.at[tile, pl.ds(pl.multiple_of(h * ch, ch), ch)]

    def c_m1(j):
        return remote(DM1, j, rows(SO, j), rows(SM1, j), dev(1, x, c))

    def c_p1(j):
        return remote(DP1, j, rows(SO, j), rows(SP1, j), dev(-1, x, c))

    def c_oo(j, h):
        return remote(DOO, j, rows(SO, j), half(BO + j, h), dev(0, x, co))

    def c_m2(j):
        return remote(DM2, j, rows(SM1, j), rows(SM2, j), dev(1, x, c))

    def c_p2(j):
        return remote(DP2, j, rows(SP1, j), half(BP2 + j, c), dev(-1, x, c))

    def c_x1(j):
        return remote(DX1, j, rows(SP1, j), half(BX1 + j, c), dev(0, xo, c))

    def c_xh_m(i):
        return remote(DXH, i, rows(SM2, i), half(BXH + i, c), dev(0, xo, c))

    def c_xh_p(i):
        return remote(DXH, i, half(BP2 + 2 + i, c), half(BXH + i, c), dev(0, xo, c))

    def c_fwd(kind, tile, j, h):
        return remote(kind, j, half(tile + j, h), half(tile + j, h), dev(0, x, co))

    def normalise(j):
        loads[j].wait()
        e = stage[j]
        u = (e * lax.rsqrt(jnp.sum(e * e, axis=1, keepdims=True) + 1e-06)).astype(BF16)
        abuf[SO, pl.ds(j * ch, ch)] = u
        bbuf[BO + j, pl.ds(pl.multiple_of(c * ch, ch), ch)] = u

    normalise(0)
    ordv[c] = order_ref[...]
    normalise(2)
    pl.semaphore_wait(barrier, len(peers))

    def order_copy(k, slot, target):
        return pltpu.make_async_remote_copy(
            src_ref=order_ref, dst_ref=ordv.at[slot], send_sem=osend_sem.at[k], recv_sem=orecv_sem.at[slot],
            device_id=target, device_id_type=MESH,
        )

    order_sends = [
        order_copy(0, VO + c, dev(0, x, co)), order_copy(1, VP1, dev(-1, x, c)), order_copy(2, VM1, dev(1, x, c)),
        order_copy(3, VM2, dev(2, x, c)),
    ]
    for h in (0, 1):
        order_sends += [order_copy(4 + h, VP2 + c, dev(-2, x, h)), order_copy(6 + h, VX1 + c, dev(-1, xo, h))]
    order_sends_low = []
    for h in (0, 1):
        order_sends_low += [order_copy(8 + h, VXH + c, dev(2, xo, h)), order_copy(10 + h, VXH + c, dev(-2, xo, h))]
    for o in order_sends:
        o.start()

    @pl.when(low)
    def _():
        for o in order_sends_low:
            o.start()

    c_m1(0).start()
    normalise(1)
    c_p1(2).start()
    normalise(3)
    c_m1(1).start()
    c_p1(3).start()
    racc[...] = jnp.full(racc.shape, -1.0, F32)
    cacc[...] = jnp.full(cacc.shape, -1.0, F32)
    for j in (2, 3):
        c_m1(j).start()
        c_p1(j - 2).start()
    for j in range(NC):
        c_oo(j, c).start()

    def order_wait(slot):
        order_copy(0, slot, dev(0, x, co)).wait_recv()

    order_wait(VO + co)
    for slot in range(VP1, NV):
        order_wait(slot)

    def build_rows(slot, v):
        for j in range(NC):
            line = ordv[v, pl.ds(j, 1)].astype(F32)
            oa[slot, pl.ds(j * ch, ch)] = jnp.broadcast_to(line, (128, ch)).T

    build_rows(SO, VO + c)
    build_rows(SP1, VP1)
    build_rows(SM1, VM1)
    build_rows(SM2, VM2)
    build_rows(SP2, VP2 + c)
    xj = jnp.where(upper, 2, 0)
    for base, v, count, off in ((BO, VO, NC, 0), (BX1, VX1, NC, 0), (BP2, VP2, NC, 0), (BXH, VXH, 2, xj)):
        for j in range(count):
            for h in (0, 1):
                line = ordv[v + h, pl.ds(j + off, 1)].astype(F32)
                ob[base + j, :, h * ch : (h + 1) * ch] = jnp.broadcast_to(line, (8, ch))

    def tiles(a, slot, r0, nrows, tile, ntiles, with_columns=True):
        b = bbuf[pl.ds(tile, ntiles)].reshape(ntiles * 2 * ch, bbuf.shape[2])
        s = lax.dot_general(a, b, (((1,), (1,)), ((), ())), preferred_element_type=F32)
        r_sl = pl.ds(pl.multiple_of(r0, ch), nrows)
        o_rows = oa[slot, r_sl]
        best = racc[slot, r_sl]
        for t in range(ntiles):
            for h in (0, 1):
                k = t * 2 + h
                sk = s[:, k * ch : (k + 1) * ch]
                m = ob[tile + t, 0:1, h * ch : (h + 1) * ch] < o_rows
                best = jnp.maximum(best, jnp.where(m, sk, -1.0))
                if with_columns:
                    down = jnp.where(m, -1.0, sk).reshape(nrows // 8, 8, ch)
                    lanes = pl.ds(h * ch, ch)
                    cacc[tile + t, :, lanes] = jnp.maximum(cacc[tile + t, :, lanes], jnp.max(down, axis=0))
        racc[slot, r_sl] = best

    nrow = NC * ch

    def whole(slot, tile, with_columns=True):
        tiles(abuf[slot], slot, 0, nrow, tile, 1, with_columns)

    def first(k, _):
        jp = lax.rem(k + 2, NC)
        c_m1(k).wait_recv()
        c_m2(k).start()
        c_p1(jp).wait_recv()
        c_p2(jp).start()
        c_x1(jp).start()
        c_oo(k, co).wait_recv()
        whole(SO, BO + k, False)

        @pl.when(k >= 1)
        def _():
            jq = lax.rem(k + 1, NC)
            c_x1(jq).wait_recv()
            c_fwd(DX1O, BX1, jq, c).start()

        return 0

    lax.fori_loop(0, NC, first, 0)
    c_x1(1).wait_recv()
    c_fwd(DX1O, BX1, 1, c).start()

    def x1_step(i, _):
        j = lax.rem(i + 2, NC)
        c_fwd(DX1O, BX1, j, co).wait_recv()

        def one(slot, _):
            whole(slot, BX1 + j)
            return 0

        lax.fori_loop(SO, SM1 + 1, one, 0)
        return 0

    lax.fori_loop(0, NC, x1_step, 0)

    def second(k, _):
        jp = lax.rem(k + 2, NC)
        c_m2(k).wait_recv()
        c_p2(jp).wait_recv()
        c_fwd(DP2O, BP2, jp, c).start()

        @pl.when(jnp.logical_and(k < 2, upper))
        def _():
            c_xh_p(k).start()

        @pl.when(jnp.logical_and(k < 2, jnp.logical_not(upper)))
        def _():
            c_xh_m(k).start()

        tiles(rows(SM2, k)[...], SM2, k * ch, ch, BX1, NC)
        c_fwd(DP2O, BP2, jp, co).wait_recv()

        def one(slot, _):
            whole(slot, BP2 + jp)
            return 0

        lax.fori_loop(SO, SM1 + 1, one, 0)

        @pl.when(lax.rem(k, 2) == 1)
        def _():
            rm = jnp.where(jnp.logical_and(k == 3, low), 2, 0)
            bp = jnp.where(jnp.logical_and(k == 3, jnp.logical_not(low)), 0, 2)

            def one(t, _):
                r0 = pl.multiple_of(rm * ch, ch)
                tiles(abuf[SM2, pl.ds(r0, 2 * ch)], SM2, r0, 2 * ch, BP2 + bp + t, 1)
                return 0

            lax.fori_loop(0, 2, one, 0)

        @pl.when(jnp.logical_or(k == 1, k == 2))
        def _():
            c_xh_m(k - 1).wait_recv()
            c_fwd(DXHO, BXH, k - 1, c).start()

        @pl.when(k == 2)
        def _():
            for i in (0, 1):
                c_fwd(DXHO, BXH, i, co).wait_recv()

        @pl.when(k >= 2)
        def _():
            @pl.when(upper)
            def _():
                r0 = pl.multiple_of((k - 2) * 2 * ch, ch)
                tiles(abuf[SM2, pl.ds(r0, 2 * ch)], SM2, r0, 2 * ch, BXH, 2)

            @pl.when(jnp.logical_not(upper))
            def _():
                def one(t, _):
                    j = lax.rem(2 * k + 2 + t, NC)
                    tiles(half(BP2 + j, c)[...], SP2, j * ch, ch, BXH, 2)
                    return 0

                lax.fori_loop(0, 2, one, 0)

        return 0

    lax.fori_loop(0, NC, second, 0)

    def row_line(slot, j):
        return jnp.max(racc[slot, pl.ds(j * ch, ch)].T, axis=0, keepdims=True)

    def col_line(tile, h):
        return jnp.max(cacc[tile, :, h * ch : (h + 1) * ch], axis=0, keepdims=True)

    res[...] = jnp.full(res.shape, -1.0, F32)
    for j in range(NC):
        res[RM2, j : j + 1] = row_line(SM2, j)
        res[RP1, j : j + 1] = row_line(SP1, j)
        res[RM1, j : j + 1] = row_line(SM1, j)
        for h in (0, 1):
            extra = jnp.where(c == h, row_line(SP2, j), -1.0)
            res[RP2 + h, j : j + 1] = jnp.maximum(col_line(BP2 + j, h), extra)
            res[RX1 + h, j : j + 1] = col_line(BX1 + j, h)
    for h in (0, 1):
        for i in (0, 1):
            res[RXHM + h, pl.ds(xj + i, 1)] = col_line(BXH + i, h)

    def result_copy(src, dst, target):
        return pltpu.make_async_remote_copy(
            src_ref=res.at[src], dst_ref=resin.at[dst], send_sem=rsend_sem.at[src], recv_sem=rrecv_sem.at[dst],
            device_id=target, device_id_type=MESH,
        )

    sends = []
    for h in (0, 1):
        sends += [result_copy(RP2 + h, RP2 + c, dev(2, x, h)), result_copy(RX1 + h, RX1 + c, dev(1, xo, h))]
    sends += [
        result_copy(RM2, RM2, dev(-2, x, c)), result_copy(RP1, RP1, dev(1, x, c)), result_copy(RM1, RM1, dev(-1, x, c))
    ]
    for s in sends:
        s.start()

    @pl.when(upper)
    def _():
        for h in (0, 1):
            result_copy(RXHM + h, RXHP + c, dev(2, xo, h)).start()

    @pl.when(jnp.logical_not(upper))
    def _():
        for h in (0, 1):
            result_copy(RXHM + h, RXHM + c, dev(-2, xo, h)).start()

    for j in range(NC):
        fin[j : j + 1] = row_line(SO, j)

    def sent(j, _):
        for copy in (c_m1, c_p1, c_m2, c_p2, c_x1):
            copy(j).wait_send()
        c_oo(j, c).wait_send()
        c_fwd(DP2O, BP2, j, c).wait_send()
        c_fwd(DX1O, BX1, j, c).wait_send()
        return 0

    lax.fori_loop(0, NC, sent, 0)
    for i in (0, 1):
        c_xh_m(i).wait_send()
        c_fwd(DXHO, BXH, i, c).wait_send()
    for o in order_sends:
        o.wait_send()

    @pl.when(low)
    def _():
        for o in order_sends_low:
            o.wait_send()

    for slot in range(RXHM):
        result_copy(0, slot, dev(1, x, c)).wait_recv()
        fin[...] = jnp.maximum(fin[...], resin[slot])

    @pl.when(low)
    def _():
        for slot in range(RXHM, NR):
            result_copy(0, slot, dev(1, x, c)).wait_recv()
            fin[...] = jnp.maximum(fin[...], resin[slot])

    for src in range(RXHM + 2):
        result_copy(src, 0, dev(1, x, c)).wait_send()
    best = fin[...]
    out_ref[0] = best
    out_ref[1] = jnp.maximum(best - thr_ref[0], 0.0)


def shards(embeddings, member_order, threshold):
    r, e = embeddings.shape
    ch = r // NC
    out = pl.pallas_call(
        kernel,
        out_shape=jax.ShapeDtypeStruct((2, NC, ch), F32),
        in_specs=[
            pl.BlockSpec(memory_space=pltpu.VMEM),
            pl.BlockSpec(memory_space=pltpu.SMEM),
            pl.BlockSpec(memory_space=pl.ANY),
        ],
        out_specs=pl.BlockSpec(memory_space=pltpu.VMEM),
        scratch_shapes=[
            pltpu.VMEM((NC, ch, e), F32),
            pltpu.VMEM((4, r, e), BF16),
            pltpu.VMEM((NB, 2 * ch, e), BF16),
            pltpu.VMEM((5, r, ch), F32),
            pltpu.VMEM((NB, 8, 2 * ch), F32),
            pltpu.VMEM((5, r, ch), F32),
            pltpu.VMEM((NB, 8, 2 * ch), F32),
            pltpu.VMEM((NV, NC, ch), jnp.int32),
            pltpu.VMEM((RXHM + 2, NC, ch), F32),
            pltpu.VMEM((NR, NC, ch), F32),
            pltpu.VMEM((NC, ch), F32),
            pltpu.SemaphoreType.DMA((NC,)),
            pltpu.SemaphoreType.DMA((ND, NC)),
            pltpu.SemaphoreType.DMA((ND, NC)),
            pltpu.SemaphoreType.DMA((12,)),
            pltpu.SemaphoreType.DMA((NV,)),
            pltpu.SemaphoreType.DMA((RXHM + 2,)),
            pltpu.SemaphoreType.DMA((NR,)),
        ],
        compiler_params=pltpu.CompilerParams(
            collective_id=0, has_side_effects=True, vmem_limit_bytes=60 * 1024 * 1024
        ),
    )(member_order.reshape(NC, ch), threshold, embeddings)
    return out[0].reshape(r), out[1].reshape(r)


def solution(mesh):
    placed = (P(("clusters", "members"), None), P(("clusters", "members")), P("clusters"))
    return jax.shard_map(
        shards,
        mesh=mesh,
        in_specs=placed,
        out_specs=(P(("clusters", "members")), P(("clusters", "members"))),
        check_vma=False,
    )
```

time: 231 us -> 73 us (0.32)
  waiting for transfers between devices: 149 us -> 0 us
  Pallas kernels: 0 us -> 70.3 us
  blocking collectives: 39.5 us -> 0 us
  matrix products: 23.2 us -> 0 us
  between operations: 14.7 us -> 1.28 us
  other arithmetic: 5.16 us -> 0 us
    all_gather x1 -> x0, waiting for transfers between devices: 149 us -> none  [shards(): lax.all_gather(unit, 'members', axis=0, tiled=True)]
    pallas_call x0 -> x1, Pallas kernels: none -> 70.3 us  [shards(): pl.pallas_call(kernel, out_shape=jax.ShapeDtypeStruct((2, NC, ch), F32),...]
    all_gather x1 -> x0, blocking collectives: 39.5 us -> none  [shards(): lax.all_gather(member_order, 'members', axis=0, tiled=True)[None, :]]
    dot_general x1 -> x0, matrix products: 23.2 us -> none  [block_scores(): lax.dot_general(unit, other, (((1,), (1,)), ((), ())), preferred_element_...]
    convert_element_type x1 -> x0, other arithmetic: 2.76 us -> none  [shards(): unit = (embeddings * lax.rsqrt(jnp.sum(embeddings * embeddings, axis=1, k...]
  transfers between devices with their start and end apart: 1 -> 0, of which waited for: 1 -> 0; matrix products, arithmetic and copies ran while one was open for 0% -> 0% of each run, Pallas kernels for 0% -> 0%
where the time goes in v1:
time: 73 us; the launch traced here: 72.8 us
  Pallas kernels  70.3 us (96%)
  between operations  1.28 us (2%)
  local copies, waits for them, and re-layouts  1.26 us (2%)
    pallas_call x1, Pallas kernels, shards(): pl.pallas_call(kernel, out_shape=jax.ShapeDtypeStruct((2, NC, ch), F32),...  70.3 us

profile of v1, /device:TPU:1, one launch (start us, length us, event | category | flops | bytes accessed | tf_op | source)
XLA Modules:
  0.0 72.8 jit_solution(9520577607391344992)
XLA Ops:
  1.3 70.3 %shard_map.50 = f32[2,4,128]{2,1,0:T(4,128)} custom-call(s32[4,128]{1,0:T(4,128)} %bitcast.5, f32[1]{0:T(128)S(6)} %copy.5.thr_ref, f32[512,1024]{1,0:T(8,128)} %emb_ref.1), custom_call_target="tpu_custom_call" | custom-call | tf_op jit(solution)/shard_map/pallas_call | solution.py:376
  71.5 1.3 %slice_bitcast_fusion = (f32[512]{0:T(512)}, f32[512]{0:T(512)}) fusion(f32[2,4,128]{2,1,0:T(4,128)} %shard_map.50), kind=kLoop, calls=%fused_computation | loop fusion | bytes 8192 | tf_op jit(solution)/shard_map/reshape;squeeze | solution.py:409

commit v2 on v0

v2 whole, which is shorter than its diff:
```python
import jax
import jax.numpy as jnp
from jax import lax
from jax.experimental import pallas as pl
from jax.experimental.pallas import tpu as pltpu
from jax.sharding import PartitionSpec as P

MESH = pl.DeviceIdType.MESH
F32 = jnp.float32
BF16 = jnp.bfloat16

SO, SP1, SM1, SM2, SP2, NS = range(6)
BO, BP1, BX1, BP2, BXH, NB = 0, 4, 8, 12, 16, 18
DM1, DP1, DOO, DM2, DP2, DX1, DXH, DP1O, DX1O, DP2O, DXHO, ND = range(12)
VO, VP1, VM1, VM2, VP2, VX1, VXH, NV = 0, 2, 4, 5, 6, 8, 10, 12
RP1, RM1, RM2, RP2, RX1, RXHM, RXHP, NR = 0, 2, 3, 4, 6, 8, 10, 12
NSRC = RXHM + 2
LANES = 128
NT = 4
SUB = 1
NC = NT * SUB


def kernel(
    order_hbm, thr_hbm, emb_ref, out_ref,
    order_ref, thr_ref, stage, abuf, bbuf, racc, cacc, oa, ob, ordv, res, resin,
    load_sem, small_sem, send_sem, recv_sem, osend_sem, orecv_sem, rsend_sem, rrecv_sem,
):
    n = lax.axis_size("members")
    nz = n // 4
    me = lax.axis_index("members")
    z, x, c = lax.div(me, 4), lax.rem(lax.div(me, 2), 2), lax.rem(me, 2)
    xo, co = 1 - x, 1 - c
    ch = abuf.shape[1] // NC

    def dev(dz, px, pc):
        return {"members": lax.rem(z + dz + nz, nz) * 4 + px * 2 + pc}

    upper = lax.rem(z + 2, nz) < nz // 2
    low = z < nz // 2

    loads = [
        pltpu.make_async_copy(emb_ref.at[pl.ds(j * ch, ch)], stage.at[j], load_sem.at[j]) for j in range(NC)
    ]
    order_in = [j + s for j in range(NC // 2) for s in (0, NC // 2)]
    for j in order_in:
        loads[j].start()
    order_load = pltpu.make_async_copy(order_hbm, order_ref, small_sem.at[0])
    order_load.start()
    thr_load = pltpu.make_async_copy(thr_hbm, thr_ref, small_sem.at[1])
    thr_load.start()

    peers = [dev(0, x, co), dev(0, xo, c)]
    for h in (0, 1):
        for dz in (2, -2, 1, -1):
            peers += [dev(dz, xo, h), dev(dz, x, h)]
    barrier = pltpu.get_barrier_semaphore()
    for p in peers:
        pl.semaphore_signal(barrier, inc=1, device_id=p, device_id_type=MESH)

    def remote(kind, j, src, dst, target):
        return pltpu.make_async_remote_copy(
            src_ref=src, dst_ref=dst, send_sem=send_sem.at[kind, j], recv_sem=recv_sem.at[kind, j],
            device_id=target, device_id_type=MESH,
        )

    def rows(slot, j):
        return abuf.at[slot, pl.ds(pl.multiple_of(j * ch, ch), ch)]

    def half(base, j, h):
        return bbuf.at[base + lax.div(j, SUB), pl.ds(pl.multiple_of(h * LANES + lax.rem(j, SUB) * ch, ch), ch)]

    def c_m1(j):
        return remote(DM1, j, rows(SO, j), rows(SM1, j), dev(1, x, c))

    def c_p1(j):
        return remote(DP1, j, rows(SO, j), rows(SP1, j), dev(-1, x, c))

    def c_m2(j):
        return remote(DM2, j, rows(SM1, j), rows(SM2, j), dev(1, x, c))

    def c_p2(j):
        return remote(DP2, j, rows(SP1, j), half(BP2, j, c), dev(-1, x, c))

    def c_x1(j):
        return remote(DX1, j, rows(SP1, j), half(BX1, j, c), dev(0, xo, c))

    def c_xh_m(i):
        return remote(DXH, i, rows(SM2, i), half(BXH, i, c), dev(0, xo, c))

    def c_xh_p(i):
        return remote(DXH, i, half(BP2, NC // 2 + i, c), half(BXH, i, c), dev(0, xo, c))

    def c_oo(j, h):
        return remote(DOO, j, rows(SO, j), half(BO, j, h), dev(0, x, co))

    def c_p1o(j, h):
        return remote(DP1O, j, rows(SP1, j), half(BP1, j, h), dev(0, x, co))

    def c_fwd(kind, base, j, h):
        return remote(kind, j, half(base, j, h), half(base, j, h), dev(0, x, co))

    def normalise(j):
        loads[j].wait()
        e = stage[j]
        u = (e * lax.rsqrt(jnp.sum(e * e, axis=1, keepdims=True) + 1e-06)).astype(BF16)
        abuf[SO, pl.ds(j * ch, ch)] = u
        bbuf[BO + j // SUB, pl.ds(pl.multiple_of(c * LANES + (j % SUB) * ch, ch), ch)] = u

    normalise(0)
    order_load.wait()
    ordv[c] = order_ref[...]
    pl.semaphore_wait(barrier, len(peers))
    def order_copy(k, slot, target):
        return pltpu.make_async_remote_copy(
            src_ref=order_ref, dst_ref=ordv.at[slot], send_sem=osend_sem.at[k], recv_sem=orecv_sem.at[slot],
            device_id=target, device_id_type=MESH,
        )

    order_sends = [order_copy(0, VO + c, dev(0, x, co)), order_copy(1, VM1, dev(1, x, c)), order_copy(2, VM2, dev(2, x, c))]
    order_sends_low = []
    for h in (0, 1):
        order_sends += [
            order_copy(3 + h, VP1 + c, dev(-1, x, h)), order_copy(5 + h, VP2 + c, dev(-2, x, h)),
            order_copy(7 + h, VX1 + c, dev(-1, xo, h)),
        ]
        order_sends_low += [order_copy(9 + h, VXH + c, dev(2, xo, h)), order_copy(11 + h, VXH + c, dev(-2, xo, h))]
    for o in order_sends:
        o.start()

    @pl.when(low)
    def _():
        for o in order_sends_low:
            o.start()

    for i in range(NC // 2):
        c_m1(i).start()
        normalise(NC // 2 + i)
        if i + 1 < NC // 2:
            normalise(i + 1)
        c_p1(NC // 2 + i).start()
    for i in range(NC // 2):
        c_m1(NC // 2 + i).start()
        c_p1(i).start()

    for j in range(NC):
        c_oo(j, c).start()
    racc[...] = jnp.full(racc.shape, -1.0, F32)
    cacc[...] = jnp.full(cacc.shape, -1.0, F32)
    res[...] = jnp.full(res.shape, -1.0, F32)

    def order_wait(slot):
        order_copy(0, slot, dev(0, x, co)).wait_recv()

    order_wait(VO + co)
    for slot in range(VP1, NV):
        order_wait(slot)

    for slot, v in ((SO, VO + c), (SP1, VP1 + c), (SM1, VM1), (SM2, VM2), (SP2, VP2 + c)):
        for j in range(NT):
            line = ordv[v, pl.ds(j, 1)].astype(F32)
            oa[slot, pl.ds(j * LANES, LANES)] = jnp.broadcast_to(line, (LANES, LANES)).T
    xj = jnp.where(upper, 2, 0)
    for base, v, count, off in ((BO, VO, NT, 0), (BP1, VP1, NT, 0), (BX1, VX1, NT, 0), (BP2, VP2, NT, 0), (BXH, VXH, 2, xj)):
        for j in range(count):
            for h in (0, 1):
                line = ordv[v + h, pl.ds(j + off, 1)].astype(F32)
                ob[base + j, :, h * LANES : (h + 1) * LANES] = jnp.broadcast_to(line, (8, LANES))

    def tiles(slot, r0, nrows, tile, ntiles, with_columns=True):
        r_sl = pl.ds(r0, nrows) if isinstance(r0, int) else pl.ds(pl.multiple_of(r0, LANES), nrows)
        b = bbuf[pl.ds(tile, ntiles)].reshape(ntiles * 2 * LANES, bbuf.shape[2])
        s = lax.dot_general(abuf[slot, r_sl], b, (((1,), (1,)), ((), ())), preferred_element_type=F32)
        o_rows = oa[slot, r_sl]
        best = racc[slot, r_sl]
        for t in range(ntiles):
            for h in (0, 1):
                k = t * 2 + h
                sk = s[:, k * LANES : (k + 1) * LANES]
                m = ob[tile + t, 0:1, h * LANES : (h + 1) * LANES] < o_rows
                best = jnp.maximum(best, jnp.where(m, sk, -1.0))
                if with_columns:
                    down = jnp.where(m, -1.0, sk).reshape(nrows // 8, 8, LANES)
                    lanes = pl.ds(h * LANES, LANES)
                    cacc[tile + t, :, lanes] = jnp.maximum(cacc[tile + t, :, lanes], jnp.max(down, axis=0))
        racc[slot, r_sl] = best

    nrow = NT * LANES
    two = 2 * LANES

    def whole(slot, tile, with_columns=True):
        tiles(slot, 0, nrow, tile, 1, with_columns)

    def loop(lo, hi, body):
        def step(i, _):
            body(i)
            return 0

        lax.fori_loop(lo, hi, step, 0)

    def turned(t):
        return lax.rem(t + NT // 2, NT)

    def subs(t):
        return [SUB * t + i for i in range(SUB)]

    def first_step(k):
        jp = lax.rem(k + NC // 2, NC)
        c_m1(k).wait_recv()
        c_m2(k).start()
        c_p1(jp).wait_recv()
        c_p2(jp).start()
        c_x1(jp).start()
        c_p1o(jp, c).start()
        half(BP1, jp, c)[...] = rows(SP1, jp)[...]

    def x1_forward(t):
        for j in subs(turned(t)):
            c_x1(j).wait_recv()
            c_fwd(DX1O, BX1, j, c).start()

    def x1_ready(t):
        for j in subs(turned(t)):
            c_fwd(DX1O, BX1, j, co).wait_recv()

    def p1_own(t):
        for j in subs(turned(t)):
            c_p1o(j, co).wait_recv()
        whole(SO, BP1 + turned(t))

    def first(kk):
        for k in subs(kk)[: max(SUB // 2, 1)]:
            first_step(k)
        for j in subs(kk):
            c_oo(j, co).wait_recv()
        whole(SO, BO + kk, False)

        @pl.when(kk >= 1)
        def _():
            p1_own(kk - 1)

        for k in subs(kk)[max(SUB // 2, 1) :]:
            first_step(k)

        @pl.when(kk >= 1)
        def _():
            x1_forward(kk - 1)

        @pl.when(kk >= 2)
        def _():
            x1_ready(kk - 2)
            whole(SO, BX1 + turned(kk - 2))

    loop(0, NT, first)
    p1_own(NT - 1)
    loop(0, NT, lambda t: whole(SM1, BP1 + t))

    def second_step(k):
        jp = lax.rem(k + NC // 2, NC)
        c_m2(k).wait_recv()
        c_p2(jp).wait_recv()
        c_fwd(DP2O, BP2, jp, c).start()

        @pl.when(jnp.logical_and(k < NC // 2, upper))
        def _():
            c_xh_p(k).start()

        @pl.when(jnp.logical_and(k < NC // 2, jnp.logical_not(upper)))
        def _():
            c_xh_m(k).start()

        rows(SP2, jp)[...] = half(BP2, jp, c)[...]

    def half_rows(q):
        slot = jnp.where(upper, SM2, SP2)
        tiles(slot, jnp.where(upper, q, 1 - q) * two, two, BXH, 2)

    def row_line(slot, j):
        return jnp.max(racc[slot, pl.ds(j * LANES, LANES)].T, axis=0, keepdims=True)

    def col_line(tile, h):
        return jnp.max(cacc[tile, :, h * LANES : (h + 1) * LANES], axis=0, keepdims=True)

    def result_copy(src, dst, target):
        return pltpu.make_async_remote_copy(
            src_ref=res.at[src], dst_ref=resin.at[dst], send_sem=rsend_sem.at[src], recv_sem=rrecv_sem.at[dst],
            device_id=target, device_id_type=MESH,
        )

    def both_halves(dst, base, slot):
        for j in range(NT):
            line = row_line(slot, j)
            for h in (0, 1):
                res[dst + h, j : j + 1] = jnp.maximum(col_line(base + j, h), jnp.where(c == h, line, -1.0))

    def second(kk):
        for k in subs(kk)[: max(SUB // 2, 1)]:
            second_step(k)

        @pl.when(kk == 0)
        def _():
            x1_ready(2)
            whole(SO, BX1 + turned(2))

            def one(i):
                whole(SP1 + lax.rem(i, 2), BX1 + turned(lax.div(i, 2)))

            loop(0, 4, one)

        @pl.when(kk == 1)
        def _():
            x1_ready(3)
            loop(SO, SM1 + 1, lambda s: whole(s, BX1 + turned(3)))

        @pl.when(kk == 2)
        def _():
            both_halves(RP1, BP1, SP1)

        @pl.when(kk == 3)
        def _():
            for h in (0, 1):
                result_copy(RP1 + h, RP1 + c, dev(1, x, h)).start()
            for i in range(NC // 2):
                c_fwd(DXHO, BXH, i, co).wait_recv()
            half_rows(0)

        for k in subs(kk)[max(SUB // 2, 1) :]:
            second_step(k)

        @pl.when(kk == 0)
        def _():
            x1_forward(3)
            loop(SP1, SM1 + 1, lambda s: whole(s, BX1 + turned(2)))

        @pl.when(jnp.logical_or(kk == 1, kk == 2))
        def _():
            for i in subs(kk - 1):
                c_xh_m(i).wait_recv()
                c_fwd(DXHO, BXH, i, c).start()

        @pl.when(lax.rem(kk, 2) == 1)
        def _():
            tiles(SM2, (kk - 1) * LANES, two, BX1, NT)

        for j in subs(turned(kk)):
            c_fwd(DP2O, BP2, j, co).wait_recv()
        whole(SM1, BP2 + turned(kk))

        @pl.when(lax.rem(kk, 2) == 1)
        def _():
            last = kk == 3
            rm = jnp.where(jnp.logical_and(last, low), two, 0)
            bp = jnp.where(jnp.logical_and(last, jnp.logical_not(low)), 0, 2)
            tiles(SM2, rm, two, BP2 + bp, 2)

    loop(0, NT, second)
    half_rows(1)

    for j in range(NT):
        res[RM2, j : j + 1] = row_line(SM2, j)
    both_halves(RP2, BP2, SP2)
    for j in range(NT):
        for h in (0, 1):
            res[RX1 + h, j : j + 1] = col_line(BX1 + j, h)
        res[RM1, j : j + 1] = row_line(SM1, j)
    for h in (0, 1):
        for i in (0, 1):
            res[RXHM + h, pl.ds(xj + i, 1)] = col_line(BXH + i, h)

    result_copy(RM2, RM2, dev(-2, x, c)).start()
    for h in (0, 1):
        result_copy(RP2 + h, RP2 + c, dev(2, x, h)).start()
        result_copy(RX1 + h, RX1 + c, dev(1, xo, h)).start()

    @pl.when(upper)
    def _():
        for h in (0, 1):
            result_copy(RXHM + h, RXHP + c, dev(2, xo, h)).start()

    @pl.when(jnp.logical_not(upper))
    def _():
        for h in (0, 1):
            result_copy(RXHM + h, RXHM + c, dev(-2, xo, h)).start()

    result_copy(RM1, RM1, dev(-1, x, c)).start()

    for j in range(NT):
        out_ref[0, j : j + 1] = row_line(SO, j)

    def sent(j):
        for copy in (c_m1, c_p1, c_m2, c_p2, c_x1):
            copy(j).wait_send()
        c_oo(j, c).wait_send()
        c_p1o(j, c).wait_send()
        c_fwd(DP2O, BP2, j, c).wait_send()
        c_fwd(DX1O, BX1, j, c).wait_send()

    loop(0, NC, sent)
    for i in range(NC // 2):
        c_xh_m(i).wait_send()
        c_fwd(DXHO, BXH, i, c).wait_send()
    for o in order_sends:
        o.wait_send()

    @pl.when(low)
    def _():
        for o in order_sends_low:
            o.wait_send()

    for slot in range(RXHM):
        result_copy(0, slot, dev(1, x, c)).wait_recv()
    thr_load.wait()
    best = out_ref[0]
    for slot in range(RXHM):
        best = jnp.maximum(best, resin[slot])
    out_ref[0] = best
    out_ref[1] = jnp.maximum(best - thr_ref[...], 0.0)

    @pl.when(low)
    def _():
        for slot in range(RXHM, NR):
            result_copy(0, slot, dev(1, x, c)).wait_recv()
        more = out_ref[0]
        for slot in range(RXHM, NR):
            more = jnp.maximum(more, resin[slot])
        out_ref[0] = more
        out_ref[1] = jnp.maximum(more - thr_ref[...], 0.0)

    for src in range(NSRC):
        result_copy(src, 0, dev(1, x, c)).wait_send()


def shards(embeddings, member_order, threshold):
    r, e = embeddings.shape
    out = pl.pallas_call(
        kernel,
        out_shape=jax.ShapeDtypeStruct((2, NT, LANES), F32),
        in_specs=[pl.BlockSpec(memory_space=pl.ANY)] * 3,
        out_specs=pl.BlockSpec(memory_space=pltpu.VMEM),
        scratch_shapes=[
            pltpu.VMEM((NT, LANES), jnp.int32),
            pltpu.VMEM((1, 1), F32),
            pltpu.VMEM((NC, r // NC, e), F32),
            pltpu.VMEM((NS, r, e), BF16),
            pltpu.VMEM((NB, 2 * LANES, e), BF16),
            pltpu.VMEM((NS, r, LANES), F32),
            pltpu.VMEM((NB, 8, 2 * LANES), F32),
            pltpu.VMEM((NS, r, LANES), F32),
            pltpu.VMEM((NB, 8, 2 * LANES), F32),
            pltpu.VMEM((NV, NT, LANES), jnp.int32),
            pltpu.VMEM((NSRC, NT, LANES), F32),
            pltpu.VMEM((NR, NT, LANES), F32),
            pltpu.SemaphoreType.DMA((NC,)),
            pltpu.SemaphoreType.DMA((2,)),
            pltpu.SemaphoreType.DMA((ND, NC)),
            pltpu.SemaphoreType.DMA((ND, NC)),
            pltpu.SemaphoreType.DMA((13,)),
            pltpu.SemaphoreType.DMA((NV,)),
            pltpu.SemaphoreType.DMA((NSRC,)),
            pltpu.SemaphoreType.DMA((NR,)),
        ],
        compiler_params=pltpu.CompilerParams(
            collective_id=0, has_side_effects=True, vmem_limit_bytes=52 * 1024 * 1024
        ),
    )(member_order.reshape(NT, LANES), threshold.reshape(1, 1), embeddings)
    return out[0].reshape(r), out[1].reshape(r)


def solution(mesh):
    placed = (P(("clusters", "members"), None), P(("clusters", "members")), P("clusters"))
    return jax.shard_map(
        shards,
        mesh=mesh,
        in_specs=placed,
        out_specs=(P(("clusters", "members")), P(("clusters", "members"))),
        check_vma=False,
    )
```

time: 231 us -> 66.9 us (0.29)
  waiting for transfers between devices: 149 us -> 0 us
  Pallas kernels: 0 us -> 64.2 us
  blocking collectives: 39.5 us -> 0 us
  matrix products: 23.2 us -> 0 us
  between operations: 14.7 us -> 1.29 us
  other arithmetic: 5.16 us -> 0 us
    all_gather x1 -> x0, waiting for transfers between devices: 149 us -> none  [shards(): lax.all_gather(unit, 'members', axis=0, tiled=True)]
    pallas_call x0 -> x1, Pallas kernels: none -> 64.2 us  [shards(): pl.pallas_call(kernel, out_shape=jax.ShapeDtypeStruct((2, NT, LANES), F32...]
    all_gather x1 -> x0, blocking collectives: 39.5 us -> none  [shards(): lax.all_gather(member_order, 'members', axis=0, tiled=True)[None, :]]
    dot_general x1 -> x0, matrix products: 23.2 us -> none  [block_scores(): lax.dot_general(unit, other, (((1,), (1,)), ((), ())), preferred_element_...]
    convert_element_type x1 -> x0, other arithmetic: 2.76 us -> none  [shards(): unit = (embeddings * lax.rsqrt(jnp.sum(embeddings * embeddings, axis=1, k...]
  transfers between devices with their start and end apart: 1 -> 0, of which waited for: 1 -> 0; matrix products, arithmetic and copies ran while one was open for 0% -> 0% of each run, Pallas kernels for 0% -> 0%
where the time goes in v2:
time: 66.9 us; the launch traced here: 66.7 us
  Pallas kernels  64.2 us (96%)
  between operations  1.29 us (2%)
  local copies, waits for them, and re-layouts  1.26 us (2%)
    pallas_call x1, Pallas kernels, shards(): pl.pallas_call(kernel, out_shape=jax.ShapeDtypeStruct((2, NT, LANES), F32...  64.2 us

profile of v2, /device:TPU:1, one launch (start us, length us, event | category | flops | bytes accessed | tf_op | source)
XLA Modules:
  0.0 66.7 jit_solution(1291148782411355882)
XLA Ops:
  1.3 0.0 copy-start
  1.3 0.7 %copy-done = s32[512]{0:T(512)S(1)} copy-done((s32[512]{0:T(512)S(1)}, s32[512]{0:T(512)}, u32[]{:S(2)}) %copy-start) | copy-done | bytes 2072
  2.0 64.2 %shard_map.50 = f32[2,4,128]{2,1,0:T(4,128)S(1)} custom-call(s32[4,128]{1,0:T(4,128)S(1)} %bitcast.7, f32[1,1]{1,0:T(1,128)} %bitcast.6.thr_hbm, f32[512,1024]{1,0:T(8,128)} %emb_ref.1), custom_call_target="tpu_custom_call" | custom-call | tf_op jit(solution)/shard_map/pallas_call | solution.py:435
  66.2 0.6 slice_bitcast_fusion
Async XLA Ops:
  1.3 0.7 %copy-start = (s32[512]{0:T(512)S(1)}, s32[512]{0:T(512)}, u32[]{:S(2)}) copy-start(s32[512]{0:T(512)} %param.4) | copy-start | bytes 6148

commit v3 on v2

--- a/solution.py
+++ b/solution.py
@@ -11,7 +11,7 @@
 
 SO, SP1, SM1, SM2, SP2, NS = range(6)
 BO, BP1, BX1, BP2, BXH, NB = 0, 4, 8, 12, 16, 18
-DM1, DP1, DOO, DM2, DP2, DX1, DXH, DP1O, DX1O, DP2O, DXHO, ND = range(12)
+DM1, DP1, DM2, DP2, DX1, DP1O, DX1O, DP2O, DXH, DOO, DXHO, ND = range(12)
 VO, VP1, VM1, VM2, VP2, VX1, VXH, NV = 0, 2, 4, 5, 6, 8, 10, 12
 RP1, RM1, RM2, RP2, RX1, RXHM, RXHP, NR = 0, 2, 3, 4, 6, 8, 10, 12
 NSRC = RXHM + 2
@@ -24,7 +24,7 @@
 def kernel(
     order_hbm, thr_hbm, emb_ref, out_ref,
     order_ref, thr_ref, stage, abuf, bbuf, racc, cacc, oa, ob, ordv, res, resin,
-    load_sem, small_sem, send_sem, recv_sem, osend_sem, orecv_sem, rsend_sem, rrecv_sem,
+    load_sem, small_sem, send_sem, recv_sem, vec_sem, orecv_sem,
 ):
     n = lax.axis_size("members")
     nz = n // 4
@@ -50,19 +50,21 @@
     thr_load = pltpu.make_async_copy(thr_hbm, thr_ref, small_sem.at[1])
     thr_load.start()
 
-    peers = [dev(0, x, co), dev(0, xo, c)]
-    for h in (0, 1):
-        for dz in (2, -2, 1, -1):
-            peers += [dev(dz, xo, h), dev(dz, x, h)]
+    peers = [dev(0, xo, c), dev(1, x, c), dev(-1, x, c), dev(0, x, co)]
     barrier = pltpu.get_barrier_semaphore()
     for p in peers:
         pl.semaphore_signal(barrier, inc=1, device_id=p, device_id_type=MESH)
 
     def remote(kind, j, src, dst, target):
+        at = kind * NC + j if kind <= DXH else DXH * NC + NC // 2 + kind - DOO
         return pltpu.make_async_remote_copy(
-            src_ref=src, dst_ref=dst, send_sem=send_sem.at[kind, j], recv_sem=recv_sem.at[kind, j],
+            src_ref=src, dst_ref=dst, send_sem=send_sem.at[kind], recv_sem=recv_sem.at[at],
             device_id=target, device_id_type=MESH,
         )
+
+    def all_of(kind, count):
+        some = abuf.at[SO, pl.ds(0, count * ch)]
+        return remote(kind, 0, some, some, dev(0, x, co))
 
     def rows(slot, j):
         return abuf.at[slot, pl.ds(pl.multiple_of(j * ch, ch), ch)]
@@ -111,33 +113,29 @@
     order_load.wait()
     ordv[c] = order_ref[...]
     pl.semaphore_wait(barrier, len(peers))
-    def order_copy(k, slot, target):
+
+    def order_copy(k, src, dst, target):
         return pltpu.make_async_remote_copy(
-            src_ref=order_ref, dst_ref=ordv.at[slot], send_sem=osend_sem.at[k], recv_sem=orecv_sem.at[slot],
+            src_ref=src, dst_ref=ordv.at[dst], send_sem=vec_sem.at[k], recv_sem=orecv_sem.at[dst],
             device_id=target, device_id_type=MESH,
         )
 
-    order_sends = [order_copy(0, VO + c, dev(0, x, co)), order_copy(1, VM1, dev(1, x, c)), order_copy(2, VM2, dev(2, x, c))]
-    order_sends_low = []
-    for h in (0, 1):
-        order_sends += [
-            order_copy(3 + h, VP1 + c, dev(-1, x, h)), order_copy(5 + h, VP2 + c, dev(-2, x, h)),
-            order_copy(7 + h, VX1 + c, dev(-1, xo, h)),
-        ]
-        order_sends_low += [order_copy(9 + h, VXH + c, dev(2, xo, h)), order_copy(11 + h, VXH + c, dev(-2, xo, h))]
-    for o in order_sends:
-        o.start()
-
-    @pl.when(low)
-    def _():
-        for o in order_sends_low:
-            o.start()
-
-    for i in range(NC // 2):
+    def order_wait(slot):
+        order_copy(0, order_ref, slot, dev(0, x, co)).wait_recv()
+
+    def order_fwd(slot):
+        order_copy(0, ordv.at[slot], slot, dev(0, x, co)).start()
+
+    order_copy(0, order_ref, VM1, dev(1, x, c)).start()
+    order_copy(0, order_ref, VP1 + c, dev(-1, x, c)).start()
+    order_copy(0, order_ref, VO + c, dev(0, x, co)).start()
+    c_m1(0).start()
+    normalise(NC // 2)
+    c_p1(NC // 2).start()
+    for i in range(1, NC // 2):
+        normalise(i)
         c_m1(i).start()
         normalise(NC // 2 + i)
-        if i + 1 < NC // 2:
-            normalise(i + 1)
         c_p1(NC // 2 + i).start()
     for i in range(NC // 2):
         c_m1(NC // 2 + i).start()
@@ -149,23 +147,35 @@
     cacc[...] = jnp.full(cacc.shape, -1.0, F32)
     res[...] = jnp.full(res.shape, -1.0, F32)
 
-    def order_wait(slot):
-        order_copy(0, slot, dev(0, x, co)).wait_recv()
-
-    order_wait(VO + co)
-    for slot in range(VP1, NV):
-        order_wait(slot)
-
-    for slot, v in ((SO, VO + c), (SP1, VP1 + c), (SM1, VM1), (SM2, VM2), (SP2, VP2 + c)):
+    order_wait(VM1)
+    order_copy(0, ordv.at[VM1], VM2, dev(1, x, c)).start()
+    order_wait(VP1 + c)
+    order_copy(0, ordv.at[VP1 + c], VP2 + c, dev(-1, x, c)).start()
+    order_copy(0, ordv.at[VP1 + c], VX1 + c, dev(0, xo, c)).start()
+    order_fwd(VP1 + c)
+    order_wait(VX1 + c)
+    order_fwd(VX1 + c)
+    for base in (VO, VP1, VX1):
+        order_wait(base + co)
+
+    def row_orders(slot, v):
         for j in range(NT):
             line = ordv[v, pl.ds(j, 1)].astype(F32)
             oa[slot, pl.ds(j * LANES, LANES)] = jnp.broadcast_to(line, (LANES, LANES)).T
-    xj = jnp.where(upper, 2, 0)
-    for base, v, count, off in ((BO, VO, NT, 0), (BP1, VP1, NT, 0), (BX1, VX1, NT, 0), (BP2, VP2, NT, 0), (BXH, VXH, 2, xj)):
+
+    def column_orders(base, v, count=NT, off=0):
         for j in range(count):
             for h in (0, 1):
                 line = ordv[v + h, pl.ds(j + off, 1)].astype(F32)
                 ob[base + j, :, h * LANES : (h + 1) * LANES] = jnp.broadcast_to(line, (8, LANES))
+
+    row_orders(SO, VO + c)
+    row_orders(SP1, VP1 + c)
+    row_orders(SM1, VM1)
+    column_orders(BO, VO)
+    column_orders(BP1, VP1)
+    column_orders(BX1, VX1)
+    xj = jnp.where(upper, 2, 0)
 
     def tiles(slot, r0, nrows, tile, ntiles, with_columns=True):
         r_sl = pl.ds(r0, nrows) if isinstance(r0, int) else pl.ds(pl.multiple_of(r0, LANES), nrows)
@@ -231,8 +241,11 @@
     def first(kk):
         for k in subs(kk)[: max(SUB // 2, 1)]:
             first_step(k)
-        for j in subs(kk):
-            c_oo(j, co).wait_recv()
+
+        @pl.when(kk == 0)
+        def _():
+            all_of(DOO, NC).wait_recv()
+
         whole(SO, BO + kk, False)
 
         @pl.when(kk >= 1)
@@ -281,9 +294,9 @@
     def col_line(tile, h):
         return jnp.max(cacc[tile, :, h * LANES : (h + 1) * LANES], axis=0, keepdims=True)
 
-    def result_copy(src, dst, target):
+    def result_copy(src, dst, target, k=4):
         return pltpu.make_async_remote_copy(
-            src_ref=res.at[src], dst_ref=resin.at[dst], send_sem=rsend_sem.at[src], recv_sem=rrecv_sem.at[dst],
+            src_ref=res.at[src], dst_ref=resin.at[dst], send_sem=vec_sem.at[3], recv_sem=vec_sem.at[k],
             device_id=target, device_id_type=MESH,
         )
 
@@ -299,6 +312,10 @@
 
         @pl.when(kk == 0)
         def _():
+            order_wait(VM2)
+            order_wait(VP2 + c)
+            order_fwd(VP2 + c)
+            order_copy(0, ordv.at[jnp.where(upper, VP2 + c, VM2)], VXH + c, dev(0, xo, c)).start()
             x1_ready(2)
             whole(SO, BX1 + turned(2))
 
@@ -306,6 +323,10 @@
                 whole(SP1 + lax.rem(i, 2), BX1 + turned(lax.div(i, 2)))
 
             loop(0, 4, one)
+            order_wait(VP2 + co)
+            row_orders(SM2, VM2)
+            row_orders(SP2, VP2 + c)
+            column_orders(BP2, VP2)
 
         @pl.when(kk == 1)
         def _():
@@ -315,13 +336,16 @@
         @pl.when(kk == 2)
         def _():
             both_halves(RP1, BP1, SP1)
+            order_wait(VXH + c)
+            order_fwd(VXH + c)
 
         @pl.when(kk == 3)
         def _():
+            order_wait(VXH + co)
+            column_orders(BXH, VXH, 2, xj)
             for h in (0, 1):
                 result_copy(RP1 + h, RP1 + c, dev(1, x, h)).start()
-            for i in range(NC // 2):
-                c_fwd(DXHO, BXH, i, co).wait_recv()
+            all_of(DXHO, NC // 2).wait_recv()
             half_rows(0)
 
         for k in subs(kk)[max(SUB // 2, 1) :]:
@@ -342,19 +366,23 @@
         def _():
             tiles(SM2, (kk - 1) * LANES, two, BX1, NT)
 
+        @pl.when(kk == 3)
+        def _():
+            half_rows(1)
+
+        @pl.when(jnp.logical_and(kk == 3, low))
+        def _():
+            tiles(SM2, two, two, BP2 + 2, 2)
+
         for j in subs(turned(kk)):
             c_fwd(DP2O, BP2, j, co).wait_recv()
         whole(SM1, BP2 + turned(kk))
 
-        @pl.when(lax.rem(kk, 2) == 1)
-        def _():
-            last = kk == 3
-            rm = jnp.where(jnp.logical_and(last, low), two, 0)
-            bp = jnp.where(jnp.logical_and(last, jnp.logical_not(low)), 0, 2)
-            tiles(SM2, rm, two, BP2 + bp, 2)
+        @pl.when(jnp.logical_or(kk == 1, jnp.logical_and(kk == 3, jnp.logical_not(low))))
+        def _():
+            tiles(SM2, 0, two, BP2 + jnp.where(kk == 1, 2, 0), 2)
 
     loop(0, NT, second)
-    half_rows(1)
 
     for j in range(NT):
         res[RM2, j : j + 1] = row_line(SM2, j)
@@ -375,40 +403,26 @@
     @pl.when(upper)
     def _():
         for h in (0, 1):
-            result_copy(RXHM + h, RXHP + c, dev(2, xo, h)).start()
+            result_copy(RXHM + h, RXHP + c, dev(2, xo, h), 5).start()
 
     @pl.when(jnp.logical_not(upper))
     def _():
         for h in (0, 1):
-            result_copy(RXHM + h, RXHM + c, dev(-2, xo, h)).start()
+            result_copy(RXHM + h, RXHM + c, dev(-2, xo, h), 5).start()
 
     result_copy(RM1, RM1, dev(-1, x, c)).start()
 
     for j in range(NT):
         out_ref[0, j : j + 1] = row_line(SO, j)
 
-    def sent(j):
-        for copy in (c_m1, c_p1, c_m2, c_p2, c_x1):
-            copy(j).wait_send()
-        c_oo(j, c).wait_send()
-        c_p1o(j, c).wait_send()
-        c_fwd(DP2O, BP2, j, c).wait_send()
-        c_fwd(DX1O, BX1, j, c).wait_send()
-
-    loop(0, NC, sent)
-    for i in range(NC // 2):
-        c_xh_m(i).wait_send()
-        c_fwd(DXHO, BXH, i, c).wait_send()
-    for o in order_sends:
-        o.wait_send()
-
-    @pl.when(low)
-    def _():
-        for o in order_sends_low:
-            o.wait_send()
-
-    for slot in range(RXHM):
-        result_copy(0, slot, dev(1, x, c)).wait_recv()
+    for kind in range(ND):
+        all_of(kind, NC // 2 if kind in (DXH, DXHO) else NC).wait_send()
+    some = ordv.at[pl.ds(0, 11)]
+    pltpu.make_async_remote_copy(
+        src_ref=some, dst_ref=some, send_sem=vec_sem.at[0], recv_sem=orecv_sem.at[0],
+        device_id=dev(0, x, co), device_id_type=MESH,
+    ).wait_send()
+    result_copy(pl.ds(0, RXHM), pl.ds(0, RXHM), dev(1, x, c)).wait_recv()
     thr_load.wait()
     best = out_ref[0]
     for slot in range(RXHM):
@@ -418,16 +432,14 @@
 
     @pl.when(low)
     def _():
-        for slot in range(RXHM, NR):
-            result_copy(0, slot, dev(1, x, c)).wait_recv()
+        result_copy(pl.ds(0, NR - RXHM), pl.ds(RXHM, NR - RXHM), dev(1, x, c), 5).wait_recv()
         more = out_ref[0]
         for slot in range(RXHM, NR):
             more = jnp.maximum(more, resin[slot])
         out_ref[0] = more
         out_ref[1] = jnp.maximum(more - thr_ref[...], 0.0)
 
-    for src in range(NSRC):
-        result_copy(src, 0, dev(1, x, c)).wait_send()
+    result_copy(pl.ds(0, NSRC), pl.ds(0, NSRC), dev(1, x, c)).wait_send()
 
 
 def shards(embeddings, member_order, threshold):
@@ -452,12 +464,10 @@
             pltpu.VMEM((NR, NT, LANES), F32),
             pltpu.SemaphoreType.DMA((NC,)),
             pltpu.SemaphoreType.DMA((2,)),
-            pltpu.SemaphoreType.DMA((ND, NC)),
-            pltpu.SemaphoreType.DMA((ND, NC)),
-            pltpu.SemaphoreType.DMA((13,)),
+            pltpu.SemaphoreType.DMA((ND,)),
+            pltpu.SemaphoreType.DMA((DXH * NC + NC // 2 + 2,)),
+            pltpu.SemaphoreType.DMA((6,)),
             pltpu.SemaphoreType.DMA((NV,)),
-            pltpu.SemaphoreType.DMA((NSRC,)),
-            pltpu.SemaphoreType.DMA((NR,)),
         ],
         compiler_params=pltpu.CompilerParams(
             collective_id=0, has_side_effects=True, vmem_limit_bytes=52 * 1024 * 1024

time: 66.9 us -> 64.8 us (0.969)
  Pallas kernels: 64.2 us -> 62.1 us
    pallas_call x1, Pallas kernels: 64.2 us -> 62.1 us  [shards(): pl.pallas_call(kernel, out_shape=jax.ShapeDtypeStruct((2, NT, LANES), F32...]
where the time goes in v3:
time: 64.8 us; the launch traced here: 64.7 us
  Pallas kernels  62.1 us (96%)
  between operations  1.29 us (2%)
  local copies, waits for them, and re-layouts  1.26 us (2%)
    pallas_call x1, Pallas kernels, shards(): pl.pallas_call(kernel, out_shape=jax.ShapeDtypeStruct((2, NT, LANES), F32...  62.1 us

profile of v3, /device:TPU:1, one launch (start us, length us, event | category | flops | bytes accessed | tf_op | source)
XLA Modules:
  0.0 64.7 jit_solution(14389786677248246613)
XLA Ops:
  1.3 0.0 copy-start
  1.3 0.7 %copy-done = s32[512]{0:T(512)S(1)} copy-done((s32[512]{0:T(512)S(1)}, s32[512]{0:T(512)}, u32[]{:S(2)}) %copy-start) | copy-done | bytes 2072
  2.0 62.1 %shard_map.50 = f32[2,4,128]{2,1,0:T(4,128)S(1)} custom-call(s32[4,128]{1,0:T(4,128)S(1)} %bitcast.7, f32[1,1]{1,0:T(1,128)} %bitcast.6.thr_hbm, f32[512,1024]{1,0:T(8,128)} %emb_ref.1), custom_call_target="tpu_custom_call" | custom-call | tf_op jit(solution)/shard_map/pallas_call | solution.py:447
  64.1 0.6 slice_bitcast_fusion
Async XLA Ops:
  1.3 0.7 %copy-start = (s32[512]{0:T(512)S(1)}, s32[512]{0:T(512)}, u32[]{:S(2)}) copy-start(s32[512]{0:T(512)} %param.4) | copy-start | bytes 6148

commit v4 on v3

--- a/solution.py
+++ b/solution.py
@@ -10,10 +10,10 @@
 BF16 = jnp.bfloat16
 
 SO, SP1, SM1, SM2, SP2, NS = range(6)
-BO, BP1, BX1, BP2, BXH, NB = 0, 4, 8, 12, 16, 18
-DM1, DP1, DM2, DP2, DX1, DP1O, DX1O, DP2O, DXH, DOO, DXHO, ND = range(12)
-VO, VP1, VM1, VM2, VP2, VX1, VXH, NV = 0, 2, 4, 5, 6, 8, 10, 12
-RP1, RM1, RM2, RP2, RX1, RXHM, RXHP, NR = 0, 2, 3, 4, 6, 8, 10, 12
+BO, BP1, BX1, BM1, BXH, BQ, NB = 0, 4, 8, 12, 16, 18, 20
+DM1, DP1, DM2, DP2, DX1, DP1O, DX1O, DXH, DOO, DM1O, DXHO, DQO, ND = range(13)
+VO, VP1, VM1, VM2, VP2, VX1, VXH, NV = 0, 2, 4, 6, 8, 10, 12, 14
+RP1, RM1, RM2, RP2, RX1, RXHM, RXHP, NR = 0, 2, 4, 6, 8, 10, 12, 14
 NSRC = RXHM + 2
 LANES = 128
 NT = 4
@@ -82,7 +82,7 @@
         return remote(DM2, j, rows(SM1, j), rows(SM2, j), dev(1, x, c))
 
     def c_p2(j):
-        return remote(DP2, j, rows(SP1, j), half(BP2, j, c), dev(-1, x, c))
+        return remote(DP2, j, rows(SP1, j), rows(SP2, j), dev(-1, x, c))
 
     def c_x1(j):
         return remote(DX1, j, rows(SP1, j), half(BX1, j, c), dev(0, xo, c))
@@ -91,13 +91,22 @@
         return remote(DXH, i, rows(SM2, i), half(BXH, i, c), dev(0, xo, c))
 
     def c_xh_p(i):
-        return remote(DXH, i, half(BP2, NC // 2 + i, c), half(BXH, i, c), dev(0, xo, c))
+        return remote(DXH, i, rows(SP2, NC // 2 + i), half(BXH, i, c), dev(0, xo, c))
 
     def c_oo(j, h):
         return remote(DOO, j, rows(SO, j), half(BO, j, h), dev(0, x, co))
 
     def c_p1o(j, h):
         return remote(DP1O, j, rows(SP1, j), half(BP1, j, h), dev(0, x, co))
+
+    def c_m1o(j, h):
+        return remote(DM1O, j, rows(SM1, j), half(BM1, j, h), dev(0, x, co))
+
+    q_slot = jnp.where(low, SP2, SM2)
+    q_off = jnp.where(low, NC // 2, 0)
+
+    def c_qo(i, h):
+        return remote(DQO, i, rows(q_slot, q_off + i), half(BQ, i, h), dev(0, x, co))
 
     def c_fwd(kind, base, j, h):
         return remote(kind, j, half(base, j, h), half(base, j, h), dev(0, x, co))
@@ -126,7 +135,7 @@
     def order_fwd(slot):
         order_copy(0, ordv.at[slot], slot, dev(0, x, co)).start()
 
-    order_copy(0, order_ref, VM1, dev(1, x, c)).start()
+    order_copy(0, order_ref, VM1 + c, dev(1, x, c)).start()
     order_copy(0, order_ref, VP1 + c, dev(-1, x, c)).start()
     order_copy(0, order_ref, VO + c, dev(0, x, co)).start()
     c_m1(0).start()
@@ -147,15 +156,16 @@
     cacc[...] = jnp.full(cacc.shape, -1.0, F32)
     res[...] = jnp.full(res.shape, -1.0, F32)
 
-    order_wait(VM1)
-    order_copy(0, ordv.at[VM1], VM2, dev(1, x, c)).start()
+    order_wait(VM1 + c)
+    order_copy(0, ordv.at[VM1 + c], VM2 + c, dev(1, x, c)).start()
+    order_fwd(VM1 + c)
     order_wait(VP1 + c)
     order_copy(0, ordv.at[VP1 + c], VP2 + c, dev(-1, x, c)).start()
     order_copy(0, ordv.at[VP1 + c], VX1 + c, dev(0, xo, c)).start()
     order_fwd(VP1 + c)
     order_wait(VX1 + c)
     order_fwd(VX1 + c)
-    for base in (VO, VP1, VX1):
+    for base in (VO, VP1, VM1, VX1):
         order_wait(base + co)
 
     def row_orders(slot, v):
@@ -171,7 +181,8 @@
 
     row_orders(SO, VO + c)
     row_orders(SP1, VP1 + c)
-    row_orders(SM1, VM1)
+    row_orders(SM1, VM1 + c)
+    column_orders(BM1, VM1)
     column_orders(BO, VO)
     column_orders(BP1, VP1)
     column_orders(BX1, VX1)
@@ -218,6 +229,8 @@
         jp = lax.rem(k + NC // 2, NC)
         c_m1(k).wait_recv()
         c_m2(k).start()
+        c_m1o(k, c).start()
+        half(BM1, k, c)[...] = rows(SM1, k)[...]
         c_p1(jp).wait_recv()
         c_p2(jp).start()
         c_x1(jp).start()
@@ -272,7 +285,11 @@
         jp = lax.rem(k + NC // 2, NC)
         c_m2(k).wait_recv()
         c_p2(jp).wait_recv()
-        c_fwd(DP2O, BP2, jp, c).start()
+
+        @pl.when(k < NC // 2)
+        def _():
+            c_qo(k, c).start()
+            half(BQ, k, c)[...] = rows(q_slot, q_off + k)[...]
 
         @pl.when(jnp.logical_and(k < NC // 2, upper))
         def _():
@@ -282,11 +299,13 @@
         def _():
             c_xh_m(k).start()
 
-        rows(SP2, jp)[...] = half(BP2, jp, c)[...]
 
     def half_rows(q):
         slot = jnp.where(upper, SM2, SP2)
         tiles(slot, jnp.where(upper, q, 1 - q) * two, two, BXH, 2)
+
+    def q_rows(q):
+        tiles(jnp.where(low, SM2, SP2), jnp.where(low, q, 1 - q) * two, two, BQ, 2)
 
     def row_line(slot, j):
         return jnp.max(racc[slot, pl.ds(j * LANES, LANES)].T, axis=0, keepdims=True)
@@ -312,10 +331,11 @@
 
         @pl.when(kk == 0)
         def _():
-            order_wait(VM2)
+            order_wait(VM2 + c)
             order_wait(VP2 + c)
             order_fwd(VP2 + c)
-            order_copy(0, ordv.at[jnp.where(upper, VP2 + c, VM2)], VXH + c, dev(0, xo, c)).start()
+            order_fwd(VM2 + c)
+            order_copy(0, ordv.at[jnp.where(upper, VP2, VM2) + c], VXH + c, dev(0, xo, c)).start()
             x1_ready(2)
             whole(SO, BX1 + turned(2))
 
@@ -324,9 +344,10 @@
 
             loop(0, 4, one)
             order_wait(VP2 + co)
-            row_orders(SM2, VM2)
+            order_wait(VM2 + co)
+            row_orders(SM2, VM2 + c)
             row_orders(SP2, VP2 + c)
-            column_orders(BP2, VP2)
+            column_orders(BQ, jnp.where(low, VP2, VM2), 2, jnp.where(low, 2, 0))
 
         @pl.when(kk == 1)
         def _():
@@ -336,6 +357,8 @@
         @pl.when(kk == 2)
         def _():
             both_halves(RP1, BP1, SP1)
+            for j in range(NT):
+                out_ref[0, j : j + 1] = row_line(SO, j)
             order_wait(VXH + c)
             order_fwd(VXH + c)
 
@@ -362,43 +385,26 @@
                 c_xh_m(i).wait_recv()
                 c_fwd(DXHO, BXH, i, c).start()
 
-        @pl.when(lax.rem(kk, 2) == 1)
-        def _():
-            tiles(SM2, (kk - 1) * LANES, two, BX1, NT)
-
-        @pl.when(kk == 3)
-        def _():
-            half_rows(1)
-
-        @pl.when(jnp.logical_and(kk == 3, low))
-        def _():
-            tiles(SM2, two, two, BP2 + 2, 2)
-
-        for j in subs(turned(kk)):
-            c_fwd(DP2O, BP2, j, co).wait_recv()
-        whole(SM1, BP2 + turned(kk))
-
-        @pl.when(jnp.logical_or(kk == 1, jnp.logical_and(kk == 3, jnp.logical_not(low))))
-        def _():
-            tiles(SM2, 0, two, BP2 + jnp.where(kk == 1, 2, 0), 2)
+        @pl.when(kk == 1)
+        def _():
+            all_of(DM1O, NC).wait_recv()
+            all_of(DQO, NC // 2).wait_recv()
+            tiles(SM2, 0, two, BX1, NT)
+            tiles(SP2, two, two, BM1, NT)
+            q_rows(0)
 
     loop(0, NT, second)
 
-    for j in range(NT):
-        res[RM2, j : j + 1] = row_line(SM2, j)
-    both_halves(RP2, BP2, SP2)
-    for j in range(NT):
-        for h in (0, 1):
+    tiles(SM2, two, two, BX1, NT)
+    for h in (0, 1):
+        for j in range(NT):
             res[RX1 + h, j : j + 1] = col_line(BX1 + j, h)
-        res[RM1, j : j + 1] = row_line(SM1, j)
+    half_rows(1)
     for h in (0, 1):
+        result_copy(RX1 + h, RX1 + c, dev(1, xo, h)).start()
         for i in (0, 1):
             res[RXHM + h, pl.ds(xj + i, 1)] = col_line(BXH + i, h)
-
-    result_copy(RM2, RM2, dev(-2, x, c)).start()
-    for h in (0, 1):
-        result_copy(RP2 + h, RP2 + c, dev(2, x, h)).start()
-        result_copy(RX1 + h, RX1 + c, dev(1, xo, h)).start()
+    tiles(SP2, 0, two, BM1, NT)
 
     @pl.when(upper)
     def _():
@@ -410,14 +416,25 @@
         for h in (0, 1):
             result_copy(RXHM + h, RXHM + c, dev(-2, xo, h), 5).start()
 
-    result_copy(RM1, RM1, dev(-1, x, c)).start()
+    both_halves(RM1, BM1, SM1)
+    q_rows(1)
+    for h in (0, 1):
+        result_copy(RM1 + h, RM1 + c, dev(-1, x, h)).start()
 
     for j in range(NT):
-        out_ref[0, j : j + 1] = row_line(SO, j)
+        for dst, slot in ((RM2, SM2), (RP2, SP2)):
+            res[dst + c, j : j + 1] = row_line(slot, j)
+    for h in (0, 1):
+        for i in (0, 1):
+            at, line = jnp.where(low, RP2, RM2) + h, pl.ds(jnp.where(low, 2, 0) + i, 1)
+            res[at, line] = jnp.maximum(res[at, line], col_line(BQ + i, h))
+    for h in (0, 1):
+        result_copy(RM2 + h, RM2 + c, dev(-2, x, h)).start()
+        result_copy(RP2 + h, RP2 + c, dev(2, x, h)).start()
 
     for kind in range(ND):
-        all_of(kind, NC // 2 if kind in (DXH, DXHO) else NC).wait_send()
-    some = ordv.at[pl.ds(0, 11)]
+        all_of(kind, NC // 2 if kind in (DXH, DXHO, DQO) else NC).wait_send()
+    some = ordv.at[pl.ds(0, 13)]
     pltpu.make_async_remote_copy(
         src_ref=some, dst_ref=some, send_sem=vec_sem.at[0], recv_sem=orecv_sem.at[0],
         device_id=dev(0, x, co), device_id_type=MESH,
@@ -465,7 +482,7 @@
             pltpu.SemaphoreType.DMA((NC,)),
             pltpu.SemaphoreType.DMA((2,)),
             pltpu.SemaphoreType.DMA((ND,)),
-            pltpu.SemaphoreType.DMA((DXH * NC + NC // 2 + 2,)),
+            pltpu.SemaphoreType.DMA((DXH * NC + NC // 2 + ND - DOO,)),
             pltpu.SemaphoreType.DMA((6,)),
             pltpu.SemaphoreType.DMA((NV,)),
         ],

time: 64.8 us -> 63.7 us (0.983)
  Pallas kernels: 62.1 us -> 61 us
    pallas_call x1, Pallas kernels: 62.1 us -> 61 us  [shards(): pl.pallas_call(kernel, out_shape=jax.ShapeDtypeStruct((2, NT, LANES), F32...]
where the time goes in v4:
time: 63.7 us; the launch traced here: 63.6 us
  Pallas kernels  61 us (96%)
  between operations  1.29 us (2%)
  local copies, waits for them, and re-layouts  1.26 us (2%)
    pallas_call x1, Pallas kernels, shards(): pl.pallas_call(kernel, out_shape=jax.ShapeDtypeStruct((2, NT, LANES), F32...  61 us

profile of v4, /device:TPU:1, one launch (start us, length us, event | category | flops | bytes accessed | tf_op | source)
XLA Modules:
  0.0 63.6 jit_solution(14649567169336643882)
XLA Ops:
  1.3 0.0 copy-start
  1.3 0.7 %copy-done = s32[512]{0:T(512)S(1)} copy-done((s32[512]{0:T(512)S(1)}, s32[512]{0:T(512)}, u32[]{:S(2)}) %copy-start) | copy-done | bytes 2072
  2.0 61.0 %shard_map.50 = f32[2,4,128]{2,1,0:T(4,128)S(1)} custom-call(s32[4,128]{1,0:T(4,128)S(1)} %bitcast.7, f32[1,1]{1,0:T(1,128)} %bitcast.6.thr_hbm, f32[512,1024]{1,0:T(8,128)} %emb_ref.1), custom_call_target="tpu_custom_call" | custom-call | tf_op jit(solution)/shard_map/pallas_call | solution.py:464
  63.0 0.6 slice_bitcast_fusion
Async XLA Ops:
  1.3 0.7 %copy-start = (s32[512]{0:T(512)S(1)}, s32[512]{0:T(512)}, u32[]{:S(2)}) copy-start(s32[512]{0:T(512)} %param.4) | copy-start | bytes 6148

commit v5 on v4

--- a/solution.py
+++ b/solution.py
@@ -135,12 +135,12 @@
     def order_fwd(slot):
         order_copy(0, ordv.at[slot], slot, dev(0, x, co)).start()
 
+    c_m1(0).start()
+    normalise(NC // 2)
+    c_p1(NC // 2).start()
     order_copy(0, order_ref, VM1 + c, dev(1, x, c)).start()
     order_copy(0, order_ref, VP1 + c, dev(-1, x, c)).start()
     order_copy(0, order_ref, VO + c, dev(0, x, co)).start()
-    c_m1(0).start()
-    normalise(NC // 2)
-    c_p1(NC // 2).start()
     for i in range(1, NC // 2):
         normalise(i)
         c_m1(i).start()

time: 63.7 us -> 65.5 us (1.028)
  Pallas kernels: 61 us -> 62.8 us
    pallas_call x1, Pallas kernels: 61 us -> 62.8 us  [shards(): pl.pallas_call(kernel, out_shape=jax.ShapeDtypeStruct((2, NT, LANES), F32...]
where the time goes in v5:
time: 65.5 us; the launch traced here: 65.3 us
  Pallas kernels  62.8 us (96%)
  between operations  1.29 us (2%)
  local copies, waits for them, and re-layouts  1.26 us (2%)
    pallas_call x1, Pallas kernels, shards(): pl.pallas_call(kernel, out_shape=jax.ShapeDtypeStruct((2, NT, LANES), F32...  62.8 us

profile of v5, /device:TPU:1, one launch (start us, length us, event | category | flops | bytes accessed | tf_op | source)
XLA Modules:
  0.0 65.3 jit_solution(16647259388447619398)
XLA Ops:
  1.3 0.0 copy-start
  1.3 0.7 %copy-done = s32[512]{0:T(512)S(1)} copy-done((s32[512]{0:T(512)S(1)}, s32[512]{0:T(512)}, u32[]{:S(2)}) %copy-start) | copy-done | bytes 2072
  2.0 62.8 %shard_map.50 = f32[2,4,128]{2,1,0:T(4,128)S(1)} custom-call(s32[4,128]{1,0:T(4,128)S(1)} %bitcast.7, f32[1,1]{1,0:T(1,128)} %bitcast.6.thr_hbm, f32[512,1024]{1,0:T(8,128)} %emb_ref.1), custom_call_target="tpu_custom_call" | custom-call | tf_op jit(solution)/shard_map/pallas_call | solution.py:464
  64.7 0.6 slice_bitcast_fusion
Async XLA Ops:
  1.3 0.7 %copy-start = (s32[512]{0:T(512)S(1)}, s32[512]{0:T(512)}, u32[]{:S(2)}) copy-start(s32[512]{0:T(512)} %param.4) | copy-start | bytes 6148
